TPU v7x, 32 devices: a whole 2x2x4 slice. The times are simulated.
32 devices in a mesh: zero: 2 (over core), cols: 4 (over y, x), ens: 4 (over z).
Axes of the slice: x: 2, y: 2, z: 4, core: 2. Of those that a mesh axis runs over, the one named last changes fastest.
Arguments:
- weight_gate: float32 [8192, 8192], P(('ens', 'zero'), 'cols'), parts along dimension 0, may hold values from -0.1875 to 0.1875
- moment_gate: float32 [8192, 8192], P(('ens', 'zero'), 'cols'), parts along dimension 0, may hold values from -0.125 to 0.125
- square_gate: float32 [8192, 8192], P(('ens', 'zero'), 'cols'), parts along dimension 0, may hold values from -0.125 to 0.125
- weight_up: float32 [8192, 8192], P(('ens', 'zero'), 'cols'), parts along dimension 0, may hold values from -0.1875 to 0.1875
- moment_up: float32 [8192, 8192], P(('ens', 'zero'), 'cols'), parts along dimension 0, may hold values from -0.125 to 0.125
- square_up: float32 [8192, 8192], P(('ens', 'zero'), 'cols'), parts along dimension 0, may hold values from -0.125 to 0.125
- norm_gain: float32 [8192], P(('ens', 'zero')), parts along dimension 0, may hold values from 0.25 to 1.75
Outputs:
- ready_gate: bfloat16 [8192, 8192], P('ens', 'cols'), parts along dimension 0
- ready_up: bfloat16 [8192, 8192], P('ens', 'cols'), parts along dimension 0
- factor_gate: float32 [32768], P(('ens', 'cols')), parts along dimension 0
- factor_up: float32 [32768], P(('ens', 'cols')), parts along dimension 0
There are 4 independent parts, one for each index of `ens`. A program takes and returns all parts, laid end to end along the dimension named above; each array names one. Nothing has to cross between parts.
All inputs are finite; a program needn't handle non-finite values. Where the computation divides by a largest or mean magnitude, that divisor is 1e-20 or more.
Results may differ from a plain program's by a relative error of at most 0.001.
Values may be sent and summed in bfloat16 or wider, within the bound.
A program may use at most 128 MiB of HBM per device.

v0:
```python
import functools

import jax
import jax.numpy as jnp
from jax import lax
from jax.experimental import pallas as pl
from jax.experimental.pallas import tpu as pltpu
from jax.sharding import PartitionSpec as P

MESH = pl.DeviceIdType.MESH
learn_rate = 0.2
hold_rate = 0.9
LANES = 128
SLOTS = 14
LAG = 2
BUDGET = 896
WIDE = 256
TAPER = (128, 128)
PIECES = 4


def kernel(
    n, plan, block,
    weight_gate, moment_gate, square_gate, weight_up, moment_up, square_up, gain_ref,
    ready_gate, ready_up, factor_gate, factor_up,
    held, gain_near, gain_wide, peaks, gain_sem, load_sem, peak_send, peak_recv, out_send, out_recv,
):
    rows, columns = weight_gate.shape
    steps = len(plan)
    me = lax.axis_index("zero")
    partners = [lax.rem(me + k, n) for k in range(1, n)]
    sources = ((weight_gate, moment_gate, square_gate), (weight_up, moment_up, square_up))
    readies = (ready_gate, ready_up)
    factors = (factor_gate, factor_up)

    def place(step):
        which, start, width = plan[step]
        return which, pl.ds(start, width), width

    def loads(step):
        which, span, width = place(step)
        slot = step % SLOTS
        return [
            pltpu.make_async_copy(source.at[:, span], held.at[slot, k, :, pl.ds(0, width)], load_sem.at[slot, k])
            for k, source in enumerate(sources[which])
        ]

    def swaps(step):
        width = plan[step][2]
        return [
            pltpu.make_async_remote_copy(
                src_ref=peaks.at[step, 0, :, pl.ds(0, width)],
                dst_ref=peaks.at[step, k + 1, :, pl.ds(0, width)],
                send_sem=peak_send.at[step, k],
                recv_sem=peak_recv.at[step, k],
                device_id={"zero": partner},
                device_id_type=MESH,
            )
            for k, partner in enumerate(partners)
        ]

    def sends(step):
        which, span, width = place(step)
        mine = readies[which].at[pl.ds(pl.multiple_of(me * rows, rows), rows), span]
        return [
            pltpu.make_async_remote_copy(
                src_ref=mine,
                dst_ref=mine,
                send_sem=out_send.at[step, k],
                recv_sem=out_recv.at[step, k],
                device_id={"zero": partner},
                device_id_type=MESH,
            )
            for k, partner in enumerate(partners)
        ]

    def update(step):
        slot = step % SLOTS

        def body(i, tops):
            span = pl.ds(pl.multiple_of(i * block, block), block)
            gain = gain_wide[span, :]
            new = []
            for j, top in enumerate(tops):
                lanes = pl.ds(j * LANES, LANES)
                hold = hold_rate * held[slot, 1, span, lanes] + held[slot, 2, span, lanes]
                gained = (held[slot, 0, span, lanes] - learn_rate * hold) * gain
                held[slot, 0, span, lanes] = gained
                high = jnp.max(jnp.abs(gained).reshape(block // 8, 8, LANES), axis=0)
                new.append(jnp.maximum(top, high))
            return tuple(new)

        zero = jnp.zeros((8, LANES), jnp.float32)
        tops = lax.fori_loop(0, rows // block, body, (zero,) * (plan[step][2] // LANES))
        for j, top in enumerate(tops):
            peaks[step, 0, :, pl.ds(j * LANES, LANES)] = top

    def finish(step):
        which, span, width = place(step)
        slot = step % SLOTS
        top = peaks[step, 0, :, pl.ds(0, width)]
        for k in range(1, n):
            top = jnp.maximum(top, peaks[step, k, :, pl.ds(0, width)])
        factor = jnp.max(top, axis=0, keepdims=True)
        factors[which][:, span] = factor
        scale = jnp.broadcast_to(1.0 / factor, (block, width))
        ready = readies[which]

        def body(i, carry):
            span_in = pl.ds(pl.multiple_of(i * block, block), block)
            span_out = pl.ds(pl.multiple_of(me * rows + i * block, block), block)
            ready[span_out, span] = (held[slot, 0, span_in, pl.ds(0, width)] * scale).astype(ready.dtype)
            return carry

        lax.fori_loop(0, rows // block, body, 0)

    gain_copy = pltpu.make_async_copy(gain_ref, gain_near, gain_sem)
    gain_copy.start()
    issued = 0

    def feed(waited, finished):
        nonlocal issued
        while issued < steps and issued < finished + SLOTS:
            ahead = sum(width for _, _, width in plan[waited:issued + 1])
            if ahead > BUDGET:
                break
            for copy in loads(issued):
                copy.start()
            issued += 1

    feed(0, 0)

    barrier = pltpu.get_barrier_semaphore()
    for partner in partners:
        pl.semaphore_signal(barrier, inc=1, device_id={"zero": partner}, device_id_type=MESH)

    gain_copy.wait()
    for k in range(rows // LANES):
        wide = jnp.broadcast_to(gain_near[k:k + 1, :], (LANES, LANES))
        gain_wide[pl.ds(k * LANES, LANES), :] = wide.T

    pl.semaphore_wait(barrier, n - 1)

    for step in range(steps + LAG):
        if step < steps:
            for copy in loads(step):
                copy.wait()
            feed(step + 1, max(step - LAG, 0))
            update(step)
            for copy in swaps(step):
                copy.start()
        done = step - LAG
        if done >= 0:
            for copy in swaps(done):
                copy.wait_recv()
            finish(done)
            for copy in sends(done):
                copy.start()
            feed(min(step + 1, steps), done + 1)

    for step in range(steps):
        for copy in swaps(step):
            copy.wait_send()
        for copy in sends(step):
            copy.wait()


def write_out(*refs):
    nears, fars, sem = refs[:4], refs[4:8], refs[8]
    copies = []
    for near, far in zip(nears[:2], fars[:2]):
        rows = near.shape[0] // PIECES
        for k in range(PIECES):
            span = pl.ds(k * rows, rows)
            copies.append((near.at[span], far.at[span]))
    copies += list(zip(nears[2:], fars[2:]))
    copies = [pltpu.make_async_copy(*pair, sem.at[k]) for k, pair in enumerate(copies)]
    for copy in copies:
        copy.start()
    for copy in copies:
        copy.wait()


def cut(columns):
    taper = TAPER if columns > sum(TAPER) else ()
    widths = list(taper)
    while sum(widths) < columns:
        widths.append(min(WIDE, columns - sum(widths)))
    plan = []
    for which, row in enumerate((widths, widths[::-1])):
        start = 0
        for width in row:
            plan.append((which, start, width))
            start += width
    return tuple(plan)


def solution(mesh):
    n = mesh.shape["zero"]

    def per_device(weight_gate, moment_gate, square_gate, weight_up, moment_up, square_up, norm_gain):
        rows, columns = weight_gate.shape
        plan = cut(columns)
        chunk = max(width for _, _, width in plan)
        block = 64
        steps = len(plan)
        ready = pltpu.VMEM((n * rows, columns), jnp.bfloat16)
        factor = pltpu.VMEM((1, columns), jnp.float32)
        hbm = pl.BlockSpec(memory_space=pltpu.HBM)
        vmem = pl.BlockSpec(memory_space=pltpu.VMEM)
        ready_gate, ready_up, factor_gate, factor_up = pl.pallas_call(
            functools.partial(kernel, n, plan, block),
            out_shape=(ready, ready, factor, factor),
            in_specs=[hbm] * 7,
            out_specs=(vmem,) * 4,
            scratch_shapes=[
                pltpu.VMEM((SLOTS, 3, rows, chunk), jnp.float32),
                pltpu.VMEM((rows // LANES, LANES), jnp.float32),
                pltpu.VMEM((rows, LANES), jnp.float32),
                pltpu.VMEM((steps, n, 8, chunk), jnp.float32),
                pltpu.SemaphoreType.DMA,
                pltpu.SemaphoreType.DMA((SLOTS, 3)),
                pltpu.SemaphoreType.DMA((steps, n - 1)),
                pltpu.SemaphoreType.DMA((steps, n - 1)),
                pltpu.SemaphoreType.DMA((steps, n - 1)),
                pltpu.SemaphoreType.DMA((steps, n - 1)),
            ],
            compiler_params=pltpu.CompilerParams(
                collective_id=0, has_side_effects=True, vmem_limit_bytes=46 * 2 ** 20
            ),
        )(
            weight_gate, moment_gate, square_gate, weight_up, moment_up, square_up,
            norm_gain.reshape(rows // LANES, LANES),
        )
        near = (ready_gate, ready_up, factor_gate.reshape(columns), factor_up.reshape(columns))
        return pl.pallas_call(
            write_out,
            out_shape=tuple(jax.ShapeDtypeStruct(part.shape, part.dtype) for part in near),
            in_specs=[vmem] * 4,
            out_specs=(hbm,) * 4,
            scratch_shapes=[pltpu.SemaphoreType.DMA((2 * PIECES + 2,))],
            compiler_params=pltpu.CompilerParams(vmem_limit_bytes=2 ** 20),
        )(*near)

    split = P(("ens", "zero"), "cols")
    return jax.shard_map(
        per_device,
        mesh=mesh,
        in_specs=(split,) * 6 + (P(("ens", "zero")),),
        out_specs=(P("ens", "cols"), P("ens", "cols"), P(("ens", "cols")), P(("ens", "cols"))),
        check_vma=False,
    )
```

profile of v0, /device:TPU:3, one launch (start us, length us, event | category | flops | bytes accessed | tf_op | source)
XLA Modules:
  0.0 28.2 jit_solution(5854723055234660402)
XLA Ops:
  0.6 21.6 %shard_map.102 = (bf16[2048,2048]{1,0:T(8,128)(2,1)S(1)}, bf16[2048,2048]{1,0:T(8,128)(2,1)S(1)}, f32[1,2048]{1,0:T(1,128)S(1)}, f32[1,2048]{1,0:T(1,128)S(1)}) custom-call(f32[1024,2048]{1,0:T(8,128)} %weight_gate.1, f32[1024,2048]{1,0:T(8,128)} %moment_gate.1, f32[1024,2048]{1,0:T(8,128)} %square_gate.1, f32[1024,2048]{1,0:T(8,128)} %weight_up.1, ...), custom_call_target="tpu_custom_call" | custom-call | tf_op jit(solution)/shard_map/pallas_call | solution.py:211
  22.2 5.9 %shard_map.103 = (bf16[2048,2048]{1,0:T(8,128)(2,1)}, bf16[2048,2048]{1,0:T(8,128)(2,1)}, f32[2048]{0:T(1024)}, f32[2048]{0:T(1024)}) custom-call(bf16[2048,2048]{1,0:T(8,128)(2,1)S(1)} %get-tuple-element.8.refs_0_, bf16[2048,2048]{1,0:T(8,128)(2,1)S(1)} %get-tuple-element.9.refs_1_, f32[2048]{0:T(1024)S(1)} %bitcast.3, f32[2048]{0:T(1024)S(1)} %bitcast.4), custom_call_target="tpu_custom_call" | custom-call | tf_op jit(solution)/shard_map/pallas_call | solution.py:236
where the time goes:
time: 28.3 us; the launch traced here: 28.2 us
  Pallas kernels  27.5 us (97%)
  between operations  0.64 us (2%)
    pallas_call x1, Pallas kernels, per_device(): pl.pallas_call(functools.partial(kernel, n, plan, block), out_shape=(read...  21.6 us
    pallas_call x1, Pallas kernels, per_device(): pl.pallas_call(write_out, out_shape=tuple((jax.ShapeDtypeStruct(part.shap...  5.95 us

commit v1 on v0

--- a/solution.py
+++ b/solution.py
@@ -11,11 +11,10 @@
 learn_rate = 0.2
 hold_rate = 0.9
 LANES = 128
-SLOTS = 14
-LAG = 2
-BUDGET = 896
+SLOTS = 10
+LAG_COLUMNS = 256
+BUDGET = 1024
 WIDE = 256
-TAPER = (128, 128)
 PIECES = 4
 
 
@@ -125,7 +124,7 @@
             if ahead > BUDGET:
                 break
             for copy in loads(issued):
-                copy.start()
+                copy.start(priority=1)
             issued += 1
 
     feed(0, 0)
@@ -141,22 +140,22 @@
 
     pl.semaphore_wait(barrier, n - 1)
 
-    for step in range(steps + LAG):
-        if step < steps:
-            for copy in loads(step):
-                copy.wait()
-            feed(step + 1, max(step - LAG, 0))
-            update(step)
-            for copy in swaps(step):
-                copy.start()
-        done = step - LAG
-        if done >= 0:
+    done = 0
+    for step in range(steps):
+        for copy in loads(step):
+            copy.wait()
+        feed(step + 1, done)
+        update(step)
+        for copy in swaps(step):
+            copy.start()
+        while done <= step and (step + 1 == steps or sum(width for _, _, width in plan[done + 1:step + 1]) >= LAG_COLUMNS):
             for copy in swaps(done):
                 copy.wait_recv()
             finish(done)
             for copy in sends(done):
                 copy.start()
-            feed(min(step + 1, steps), done + 1)
+            done += 1
+            feed(step + 1, done)
 
     for step in range(steps):
         for copy in swaps(step):
@@ -182,16 +181,10 @@
 
 
 def cut(columns):
-    taper = TAPER if columns > sum(TAPER) else ()
-    widths = list(taper)
-    while sum(widths) < columns:
-        widths.append(min(WIDE, columns - sum(widths)))
     plan = []
-    for which, row in enumerate((widths, widths[::-1])):
-        start = 0
-        for width in row:
-            plan.append((which, start, width))
-            start += width
+    for which in range(2):
+        for start in range(0, columns, WIDE):
+            plan.append((which, start, min(WIDE, columns - start)))
     return tuple(plan)
 
 

time: 28.3 us -> 27 us (0.954)
  Pallas kernels: 27.5 us -> 26.2 us
    pallas_call x1, Pallas kernels: 21.6 us -> 20.3 us  [per_device(): pl.pallas_call(functools.partial(kernel, n, plan, block), out_shape=(read...]
where the time goes in v1:
time: 27 us; the launch traced here: 26.8 us
  Pallas kernels  26.2 us (97%)
  between operations  0.64 us (2%)
    pallas_call x1, Pallas kernels, per_device(): pl.pallas_call(functools.partial(kernel, n, plan, block), out_shape=(read...  20.3 us
    pallas_call x1, Pallas kernels, per_device(): pl.pallas_call(write_out, out_shape=tuple((jax.ShapeDtypeStruct(part.shap...  5.95 us

profile of v1, /device:TPU:3, one launch (start us, length us, event | category | flops | bytes accessed | tf_op | source)
XLA Modules:
  0.0 26.8 jit_solution(14112099799474425583)
XLA Ops:
  0.6 20.3 %shard_map.102 = (bf16[2048,2048]{1,0:T(8,128)(2,1)S(1)}, bf16[2048,2048]{1,0:T(8,128)(2,1)S(1)}, f32[1,2048]{1,0:T(1,128)S(1)}, f32[1,2048]{1,0:T(1,128)S(1)}) custom-call(f32[1024,2048]{1,0:T(8,128)} %weight_gate.1, f32[1024,2048]{1,0:T(8,128)} %moment_gate.1, f32[1024,2048]{1,0:T(8,128)} %square_gate.1, f32[1024,2048]{1,0:T(8,128)} %weight_up.1, ...), custom_call_target="tpu_custom_call" | custom-call | tf_op jit(solution)/shard_map/pallas_call | solution.py:204
  20.9 5.9 %shard_map.103 = (bf16[2048,2048]{1,0:T(8,128)(2,1)}, bf16[2048,2048]{1,0:T(8,128)(2,1)}, f32[2048]{0:T(1024)}, f32[2048]{0:T(1024)}) custom-call(bf16[2048,2048]{1,0:T(8,128)(2,1)S(1)} %get-tuple-element.8.refs_0_, bf16[2048,2048]{1,0:T(8,128)(2,1)S(1)} %get-tuple-element.9.refs_1_, f32[2048]{0:T(1024)S(1)} %bitcast.3, f32[2048]{0:T(1024)S(1)} %bitcast.4), custom_call_target="tpu_custom_call" | custom-call | tf_op jit(solution)/shard_map/pallas_call | solution.py:229

commit v2 on v0

v2 whole, which is shorter than its diff:
```python
import functools

import jax
import jax.numpy as jnp
from jax import lax
from jax.experimental import pallas as pl
from jax.experimental.pallas import tpu as pltpu
from jax.sharding import PartitionSpec as P

MESH = pl.DeviceIdType.MESH
learn_rate = 0.2
hold_rate = 0.9
LANES = 128
SLOTS = 7
AHEAD = 4
LAG = 1
RING = 4
WIDE = 256
PIECES = 4


def kernel(
    n, plan, block,
    weight_gate, moment_gate, square_gate, weight_up, moment_up, square_up, gain_ref,
    ready_gate, ready_up, factor_gate, factor_up,
    held, gain_near, gain_wide, peaks, gain_sem, load_sem, peak_send, peak_recv, out_send, out_recv,
):
    rows, columns = weight_gate.shape
    steps = len(plan)
    width = held.shape[-1]
    me = lax.axis_index("zero")
    partners = [lax.rem(me + k, n) for k in range(1, n)]
    sources = ((weight_gate, moment_gate, square_gate), (weight_up, moment_up, square_up))
    readies = (ready_gate, ready_up)
    factors = (factor_gate, factor_up)

    def place(step):
        which, start = plan[step]
        return which, pl.ds(start, width)

    def rows_of(device):
        return pl.ds(pl.multiple_of(device * rows, rows), rows)

    def load(step):
        which, span = place(step)
        slot = step % SLOTS
        for k, source in enumerate(sources[which]):
            pltpu.make_async_copy(source.at[:, span], held.at[slot, k], load_sem.at[slot]).start(priority=1)

    def loaded(step):
        slot = step % SLOTS
        pltpu.make_async_copy(held.at[slot], held.at[slot], load_sem.at[slot]).wait()

    def to_partner(k, src, dst, send_sem, recv_sem):
        return pltpu.make_async_remote_copy(
            src_ref=src,
            dst_ref=dst,
            send_sem=send_sem,
            recv_sem=recv_sem,
            device_id={"zero": partners[k]},
            device_id_type=MESH,
        )

    def swaps(step):
        return [
            to_partner(
                k, peaks.at[0, step], peaks.at[k + 1, step], peak_send.at[k], peak_recv.at[step % RING, k]
            )
            for k in range(n - 1)
        ]

    def sends(step):
        which, span = place(step)
        mine = readies[which].at[rows_of(me), span]
        return [to_partner(k, mine, mine, out_send.at[which, k], out_recv.at[which, k]) for k in range(n - 1)]

    def update(step):
        slot = step % SLOTS

        def body(i, tops):
            span = pl.ds(pl.multiple_of(i * block, block), block)
            gain = gain_wide[span, :]
            new = []
            for j, top in enumerate(tops):
                lanes = pl.ds(j * LANES, LANES)
                hold = hold_rate * held[slot, 1, span, lanes] + held[slot, 2, span, lanes]
                gained = (held[slot, 0, span, lanes] - learn_rate * hold) * gain
                held[slot, 0, span, lanes] = gained
                high = jnp.max(jnp.abs(gained).reshape(block // 8, 8, LANES), axis=0)
                new.append(jnp.maximum(top, high))
            return tuple(new)

        zero = jnp.zeros((8, LANES), jnp.float32)
        tops = lax.fori_loop(0, rows // block, body, (zero,) * (width // LANES))
        for j, top in enumerate(tops):
            peaks[0, step, :, pl.ds(j * LANES, LANES)] = top

    def finish(step):
        which, span = place(step)
        slot = step % SLOTS
        top = peaks[0, step]
        for k in range(1, n):
            top = jnp.maximum(top, peaks[k, step])
        factor = jnp.max(top, axis=0, keepdims=True)
        factors[which][:, span] = factor
        scale = jnp.broadcast_to(1.0 / factor, (block, width))
        ready = readies[which]

        def body(i, carry):
            span_in = pl.ds(pl.multiple_of(i * block, block), block)
            span_out = pl.ds(pl.multiple_of(me * rows + i * block, block), block)
            ready[span_out, span] = (held[slot, 0, span_in, :] * scale).astype(ready.dtype)
            return carry

        lax.fori_loop(0, rows // block, body, 0)

    gain_copy = pltpu.make_async_copy(gain_ref, gain_near, gain_sem)
    gain_copy.start()
    for step in range(min(AHEAD, steps)):
        load(step)

    barrier = pltpu.get_barrier_semaphore()
    for partner in partners:
        pl.semaphore_signal(barrier, inc=1, device_id={"zero": partner}, device_id_type=MESH)

    gain_copy.wait()
    for k in range(rows // LANES):
        wide = jnp.broadcast_to(gain_near[k:k + 1, :], (LANES, LANES))
        gain_wide[pl.ds(k * LANES, LANES), :] = wide.T

    pl.semaphore_wait(barrier, n - 1)

    for step in range(steps + LAG):
        if step < steps:
            loaded(step)
            if step + AHEAD < steps:
                load(step + AHEAD)
            update(step)
            for copy in swaps(step):
                copy.start()
        done = step - LAG
        if done >= 0:
            for copy in swaps(done):
                copy.wait_recv()
            finish(done)
            for copy in sends(done):
                copy.start()

    for k, partner in enumerate(partners):
        to_partner(k, peaks.at[0], peaks.at[0], peak_send.at[k], peak_recv.at[0, k]).wait_send()
        for which, ready in enumerate(readies):
            mine = ready.at[rows_of(me)]
            copy = to_partner(k, mine, mine, out_send.at[which, k], out_recv.at[which, k])
            copy.wait()


def write_out(*refs):
    nears, fars, sem = refs[:4], refs[4:8], refs[8]
    for k, (near, far) in enumerate(zip(nears, fars)):
        pieces = PIECES if k < 2 else 1
        rows = near.shape[0] // pieces
        for piece in range(pieces):
            span = pl.ds(piece * rows, rows)
            pltpu.make_async_copy(near.at[span], far.at[span], sem.at[k]).start()
    for k, (near, far) in enumerate(zip(nears, fars)):
        pltpu.make_async_copy(near, far, sem.at[k]).wait()


def solution(mesh):
    n = mesh.shape["zero"]

    def per_device(weight_gate, moment_gate, square_gate, weight_up, moment_up, square_up, norm_gain):
        rows, columns = weight_gate.shape
        wide = WIDE if columns % WIDE == 0 else LANES
        plan = tuple((which, start) for which in range(2) for start in range(0, columns, wide))
        block = 128
        steps = len(plan)
        ready = pltpu.VMEM((n * rows, columns), jnp.bfloat16)
        factor = pltpu.VMEM((1, columns), jnp.float32)
        hbm = pl.BlockSpec(memory_space=pltpu.HBM)
        vmem = pl.BlockSpec(memory_space=pltpu.VMEM)
        ready_gate, ready_up, factor_gate, factor_up = pl.pallas_call(
            functools.partial(kernel, n, plan, block),
            out_shape=(ready, ready, factor, factor),
            in_specs=[hbm] * 7,
            out_specs=(vmem,) * 4,
            scratch_shapes=[
                pltpu.VMEM((SLOTS, 3, rows, wide), jnp.float32),
                pltpu.VMEM((rows // LANES, LANES), jnp.float32),
                pltpu.VMEM((rows, LANES), jnp.float32),
                pltpu.VMEM((n, steps, 8, wide), jnp.float32),
                pltpu.SemaphoreType.DMA,
                pltpu.SemaphoreType.DMA((SLOTS,)),
                pltpu.SemaphoreType.DMA((n - 1,)),
                pltpu.SemaphoreType.DMA((RING, n - 1)),
                pltpu.SemaphoreType.DMA((2, n - 1)),
                pltpu.SemaphoreType.DMA((2, n - 1)),
            ],
            compiler_params=pltpu.CompilerParams(
                collective_id=0, has_side_effects=True, vmem_limit_bytes=46 * 2 ** 20
            ),
        )(
            weight_gate, moment_gate, square_gate, weight_up, moment_up, square_up,
            norm_gain.reshape(rows // LANES, LANES),
        )
        near = (ready_gate, ready_up, factor_gate.reshape(columns), factor_up.reshape(columns))
        return pl.pallas_call(
            write_out,
            out_shape=tuple(jax.ShapeDtypeStruct(part.shape, part.dtype) for part in near),
            in_specs=[vmem] * 4,
            out_specs=(hbm,) * 4,
            scratch_shapes=[pltpu.SemaphoreType.DMA((4,))],
            compiler_params=pltpu.CompilerParams(vmem_limit_bytes=2 ** 20),
        )(*near)

    split = P(("ens", "zero"), "cols")
    return jax.shard_map(
        per_device,
        mesh=mesh,
        in_specs=(split,) * 6 + (P(("ens", "zero")),),
        out_specs=(P("ens", "cols"), P("ens", "cols"), P(("ens", "cols")), P(("ens", "cols"))),
        check_vma=False,
    )
```

time: 28.3 us -> 26.1 us (0.922)
  Pallas kernels: 27.5 us -> 25.3 us
    pallas_call x1, Pallas kernels: 21.6 us -> 19.4 us  [per_device(): pl.pallas_call(functools.partial(kernel, n, plan, block), out_shape=(read...]
where the time goes in v2:
time: 26.1 us; the launch traced here: 26 us
  Pallas kernels  25.3 us (97%)
  between operations  0.64 us (2%)
    pallas_call x1, Pallas kernels, per_device(): pl.pallas_call(functools.partial(kernel, n, plan, block), out_shape=(read...  19.4 us
    pallas_call x1, Pallas kernels, per_device(): pl.pallas_call(write_out, out_shape=tuple((jax.ShapeDtypeStruct(part.shap...  5.89 us

profile of v2, /device:TPU:3, one launch (start us, length us, event | category | flops | bytes accessed | tf_op | source)
XLA Modules:
  0.0 26.0 jit_solution(1815449353919786220)
XLA Ops:
  0.6 19.4 %shard_map.102 = (bf16[2048,2048]{1,0:T(8,128)(2,1)S(1)}, bf16[2048,2048]{1,0:T(8,128)(2,1)S(1)}, f32[1,2048]{1,0:T(1,128)S(1)}, f32[1,2048]{1,0:T(1,128)S(1)}) custom-call(f32[1024,2048]{1,0:T(8,128)} %weight_gate.1, f32[1024,2048]{1,0:T(8,128)} %moment_gate.1, f32[1024,2048]{1,0:T(8,128)} %square_gate.1, f32[1024,2048]{1,0:T(8,128)} %weight_up.1, ...), custom_call_target="tpu_custom_call" | custom-call | tf_op jit(solution)/shard_map/pallas_call | solution.py:182
  20.1 5.9 %shard_map.103 = (bf16[2048,2048]{1,0:T(8,128)(2,1)}, bf16[2048,2048]{1,0:T(8,128)(2,1)}, f32[2048]{0:T(1024)}, f32[2048]{0:T(1024)}) custom-call(bf16[2048,2048]{1,0:T(8,128)(2,1)S(1)} %get-tuple-element.8.refs_0_, bf16[2048,2048]{1,0:T(8,128)(2,1)S(1)} %get-tuple-element.9.refs_1_, f32[2048]{0:T(1024)S(1)} %bitcast.3, f32[2048]{0:T(1024)S(1)} %bitcast.4), custom_call_target="tpu_custom_call" | custom-call | tf_op jit(solution)/shard_map/pallas_call | solution.py:207

commit v3 on v2

--- a/solution.py
+++ b/solution.py
@@ -11,11 +11,14 @@
 learn_rate = 0.2
 hold_rate = 0.9
 LANES = 128
-SLOTS = 7
+SLOTS = 6
 AHEAD = 4
-LAG = 1
-RING = 4
+RING = 5
+UPDATE = 256 * 128
 WIDE = 256
+SPLIT = 2
+PARTS = 2
+TAPER = True
 PIECES = 4
 
 
@@ -27,7 +30,7 @@
 ):
     rows, columns = weight_gate.shape
     steps = len(plan)
-    width = held.shape[-1]
+    wide = held.shape[-1]
     me = lax.axis_index("zero")
     partners = [lax.rem(me + k, n) for k in range(1, n)]
     sources = ((weight_gate, moment_gate, square_gate), (weight_up, moment_up, square_up))
@@ -35,21 +38,26 @@
     factors = (factor_gate, factor_up)
 
     def place(step):
-        which, start = plan[step]
-        return which, pl.ds(start, width)
+        which, start, width = plan[step]
+        return which, pl.ds(start, width), width
 
     def rows_of(device):
         return pl.ds(pl.multiple_of(device * rows, rows), rows)
 
     def load(step):
-        which, span = place(step)
-        slot = step % SLOTS
-        for k, source in enumerate(sources[which]):
-            pltpu.make_async_copy(source.at[:, span], held.at[slot, k], load_sem.at[slot]).start(priority=1)
-
-    def loaded(step):
-        slot = step % SLOTS
-        pltpu.make_async_copy(held.at[slot], held.at[slot], load_sem.at[slot]).wait()
+        which, span, width = place(step)
+        slot = step % SLOTS
+        for part in range(SPLIT):
+            some = pl.ds(part * (rows // SPLIT), rows // SPLIT)
+            for k, source in enumerate(sources[which]):
+                near = held.at[slot, k, some, pl.ds(0, width)]
+                pltpu.make_async_copy(source.at[some, span], near, load_sem.at[slot, part]).start(priority=1)
+
+    def loaded(step, part):
+        slot = step % SLOTS
+        some = pl.ds(part * (rows // SPLIT), rows // SPLIT)
+        near = held.at[slot, :, some, pl.ds(0, plan[step][2])]
+        pltpu.make_async_copy(near, near, load_sem.at[slot, part]).wait()
 
     def to_partner(k, src, dst, send_sem, recv_sem):
         return pltpu.make_async_remote_copy(
@@ -62,23 +70,27 @@
         )
 
     def swaps(step):
+        lanes = pl.ds(0, plan[step][2])
+        mine = peaks.at[0, step, :, lanes]
         return [
-            to_partner(
-                k, peaks.at[0, step], peaks.at[k + 1, step], peak_send.at[k], peak_recv.at[step % RING, k]
-            )
+            to_partner(k, mine, peaks.at[k + 1, step, :, lanes], peak_send.at[k], peak_recv.at[step % RING, k])
             for k in range(n - 1)
         ]
 
-    def sends(step):
-        which, span = place(step)
-        mine = readies[which].at[rows_of(me), span]
-        return [to_partner(k, mine, mine, out_send.at[which, k], out_recv.at[which, k]) for k in range(n - 1)]
-
-    def update(step):
-        slot = step % SLOTS
+    def send(step, part):
+        which, span, _ = place(step)
+        some = rows // PARTS
+        mine = readies[which].at[pl.ds(pl.multiple_of(me * rows + part * some, some), some), span]
+        for k in range(n - 1):
+            to_partner(k, mine, mine, out_send.at[which, k], out_recv.at[which, k]).start()
+
+    def update(step, part, tops):
+        slot = step % SLOTS
+        block = min(UPDATE // plan[step][2], rows // SPLIT)
+        first = part * (rows // SPLIT)
 
         def body(i, tops):
-            span = pl.ds(pl.multiple_of(i * block, block), block)
+            span = pl.ds(pl.multiple_of(first + i * block, block), block)
             gain = gain_wide[span, :]
             new = []
             for j, top in enumerate(tops):
@@ -90,17 +102,15 @@
                 new.append(jnp.maximum(top, high))
             return tuple(new)
 
-        zero = jnp.zeros((8, LANES), jnp.float32)
-        tops = lax.fori_loop(0, rows // block, body, (zero,) * (width // LANES))
-        for j, top in enumerate(tops):
-            peaks[0, step, :, pl.ds(j * LANES, LANES)] = top
+        return lax.fori_loop(0, rows // SPLIT // block, body, tops)
 
     def finish(step):
-        which, span = place(step)
-        slot = step % SLOTS
-        top = peaks[0, step]
+        which, span, width = place(step)
+        slot = step % SLOTS
+        lanes = pl.ds(0, width)
+        top = peaks[0, step, :, lanes]
         for k in range(1, n):
-            top = jnp.maximum(top, peaks[k, step])
+            top = jnp.maximum(top, peaks[k, step, :, lanes])
         factor = jnp.max(top, axis=0, keepdims=True)
         factors[which][:, span] = factor
         scale = jnp.broadcast_to(1.0 / factor, (block, width))
@@ -109,10 +119,13 @@
         def body(i, carry):
             span_in = pl.ds(pl.multiple_of(i * block, block), block)
             span_out = pl.ds(pl.multiple_of(me * rows + i * block, block), block)
-            ready[span_out, span] = (held[slot, 0, span_in, :] * scale).astype(ready.dtype)
+            ready[span_out, span] = (held[slot, 0, span_in, lanes] * scale).astype(ready.dtype)
             return carry
 
-        lax.fori_loop(0, rows // block, body, 0)
+        count = rows // PARTS // block
+        for part in range(PARTS):
+            lax.fori_loop(part * count, (part + 1) * count, body, 0)
+            send(step, part)
 
     gain_copy = pltpu.make_async_copy(gain_ref, gain_near, gain_sem)
     gain_copy.start()
@@ -125,29 +138,32 @@
 
     gain_copy.wait()
     for k in range(rows // LANES):
-        wide = jnp.broadcast_to(gain_near[k:k + 1, :], (LANES, LANES))
-        gain_wide[pl.ds(k * LANES, LANES), :] = wide.T
+        gains = jnp.broadcast_to(gain_near[k:k + 1, :], (LANES, LANES))
+        gain_wide[pl.ds(k * LANES, LANES), :] = gains.T
 
     pl.semaphore_wait(barrier, n - 1)
 
-    for step in range(steps + LAG):
-        if step < steps:
-            loaded(step)
-            if step + AHEAD < steps:
+    done = 0
+    for step in range(steps):
+        tops = (jnp.zeros((8, LANES), jnp.float32),) * (plan[step][2] // LANES)
+        for part in range(SPLIT):
+            loaded(step, part)
+            if part + 1 == SPLIT and step + AHEAD < steps:
                 load(step + AHEAD)
-            update(step)
-            for copy in swaps(step):
-                copy.start()
-        done = step - LAG
-        if done >= 0:
+            tops = update(step, part, tops)
+        for j, top in enumerate(tops):
+            peaks[0, step, :, pl.ds(j * LANES, LANES)] = top
+        for copy in swaps(step):
+            copy.start()
+        while done < steps and (step + 1 == steps or (done < step and plan[step][2] == wide)):
             for copy in swaps(done):
                 copy.wait_recv()
             finish(done)
-            for copy in sends(done):
-                copy.start()
+            done += 1
 
     for k, partner in enumerate(partners):
-        to_partner(k, peaks.at[0], peaks.at[0], peak_send.at[k], peak_recv.at[0, k]).wait_send()
+        mine = peaks.at[0, pl.ds(0, 2 * columns // wide)]
+        to_partner(k, mine, mine, peak_send.at[k], peak_recv.at[0, k]).wait_send()
         for which, ready in enumerate(readies):
             mine = ready.at[rows_of(me)]
             copy = to_partner(k, mine, mine, out_send.at[which, k], out_recv.at[which, k])
@@ -172,8 +188,11 @@
     def per_device(weight_gate, moment_gate, square_gate, weight_up, moment_up, square_up, norm_gain):
         rows, columns = weight_gate.shape
         wide = WIDE if columns % WIDE == 0 else LANES
-        plan = tuple((which, start) for which in range(2) for start in range(0, columns, wide))
-        block = 128
+        plan = [(which, start, wide) for which in range(2) for start in range(0, columns, wide)]
+        if TAPER and wide > LANES:
+            which, start, _ = plan.pop()
+            plan += [(which, start + k, LANES) for k in range(0, wide, LANES)]
+        block = min(128, rows // PARTS)
         steps = len(plan)
         ready = pltpu.VMEM((n * rows, columns), jnp.bfloat16)
         factor = pltpu.VMEM((1, columns), jnp.float32)
@@ -190,7 +209,7 @@
                 pltpu.VMEM((rows, LANES), jnp.float32),
                 pltpu.VMEM((n, steps, 8, wide), jnp.float32),
                 pltpu.SemaphoreType.DMA,
-                pltpu.SemaphoreType.DMA((SLOTS,)),
+                pltpu.SemaphoreType.DMA((SLOTS, SPLIT)),
                 pltpu.SemaphoreType.DMA((n - 1,)),
                 pltpu.SemaphoreType.DMA((RING, n - 1)),
                 pltpu.SemaphoreType.DMA((2, n - 1)),

time: 26.1 us -> 25.9 us (level)
  no operation moved by 1% of the time
where the time goes in v3:
time: 25.9 us; the launch traced here: 25.7 us
  Pallas kernels  25.1 us (97%)
  between operations  0.64 us (2%)
    pallas_call x1, Pallas kernels, per_device(): pl.pallas_call(functools.partial(kernel, n, plan, block), out_shape=(read...  19.2 us
    pallas_call x1, Pallas kernels, per_device(): pl.pallas_call(write_out, out_shape=tuple((jax.ShapeDtypeStruct(part.shap...  5.89 us

profile of v3, /device:TPU:3, one launch (start us, length us, event | category | flops | bytes accessed | tf_op | source)
XLA Modules:
  0.0 25.7 jit_solution(8240508509538737709)
XLA Ops:
  0.6 19.2 %shard_map.102 = (bf16[2048,2048]{1,0:T(8,128)(2,1)S(1)}, bf16[2048,2048]{1,0:T(8,128)(2,1)S(1)}, f32[1,2048]{1,0:T(1,128)S(1)}, f32[1,2048]{1,0:T(1,128)S(1)}) custom-call(f32[1024,2048]{1,0:T(8,128)} %weight_gate.1, f32[1024,2048]{1,0:T(8,128)} %moment_gate.1, f32[1024,2048]{1,0:T(8,128)} %square_gate.1, f32[1024,2048]{1,0:T(8,128)} %weight_up.1, ...), custom_call_target="tpu_custom_call" | custom-call | tf_op jit(solution)/shard_map/pallas_call | solution.py:201
  19.8 5.9 %shard_map.103 = (bf16[2048,2048]{1,0:T(8,128)(2,1)}, bf16[2048,2048]{1,0:T(8,128)(2,1)}, f32[2048]{0:T(1024)}, f32[2048]{0:T(1024)}) custom-call(bf16[2048,2048]{1,0:T(8,128)(2,1)S(1)} %get-tuple-element.8.refs_0_, bf16[2048,2048]{1,0:T(8,128)(2,1)S(1)} %get-tuple-element.9.refs_1_, f32[2048]{0:T(1024)S(1)} %bitcast.3, f32[2048]{0:T(1024)S(1)} %bitcast.4), custom_call_target="tpu_custom_call" | custom-call | tf_op jit(solution)/shard_map/pallas_call | solution.py:226

commit v4 on v3

--- a/solution.py
+++ b/solution.py
@@ -11,8 +11,8 @@
 learn_rate = 0.2
 hold_rate = 0.9
 LANES = 128
-SLOTS = 6
-AHEAD = 4
+SLOTS = 5
+AHEAD = 3
 RING = 5
 UPDATE = 256 * 128
 WIDE = 256
@@ -172,7 +172,8 @@
 
 def write_out(*refs):
     nears, fars, sem = refs[:4], refs[4:8], refs[8]
-    for k, (near, far) in enumerate(zip(nears, fars)):
+    pairs = list(enumerate(zip(nears, fars)))
+    for k, (near, far) in pairs[2:] + pairs[:2]:
         pieces = PIECES if k < 2 else 1
         rows = near.shape[0] // pieces
         for piece in range(pieces):

time: 25.9 us -> 25.9 us (level)
  no operation moved by 1% of the time
where the time goes in v4:
time: 25.9 us; the launch traced here: 25.7 us
  Pallas kernels  25.1 us (97%)
  between operations  0.64 us (2%)
    pallas_call x1, Pallas kernels, per_device(): pl.pallas_call(functools.partial(kernel, n, plan, block), out_shape=(read...  19.2 us
    pallas_call x1, Pallas kernels, per_device(): pl.pallas_call(write_out, out_shape=tuple((jax.ShapeDtypeStruct(part.shap...  5.9 us

profile of v4, /device:TPU:3, one launch (start us, length us, event | category | flops | bytes accessed | tf_op | source)
XLA Modules:
  0.0 25.7 jit_solution(2257634351296737794)
XLA Ops:
  0.6 19.2 %shard_map.102 = (bf16[2048,2048]{1,0:T(8,128)(2,1)S(1)}, bf16[2048,2048]{1,0:T(8,128)(2,1)S(1)}, f32[1,2048]{1,0:T(1,128)S(1)}, f32[1,2048]{1,0:T(1,128)S(1)}) custom-call(f32[1024,2048]{1,0:T(8,128)} %weight_gate.1, f32[1024,2048]{1,0:T(8,128)} %moment_gate.1, f32[1024,2048]{1,0:T(8,128)} %square_gate.1, f32[1024,2048]{1,0:T(8,128)} %weight_up.1, ...), custom_call_target="tpu_custom_call" | custom-call | tf_op jit(solution)/shard_map/pallas_call | solution.py:202
  19.8 5.9 %shard_map.103 = (bf16[2048,2048]{1,0:T(8,128)(2,1)}, bf16[2048,2048]{1,0:T(8,128)(2,1)}, f32[2048]{0:T(1024)}, f32[2048]{0:T(1024)}) custom-call(bf16[2048,2048]{1,0:T(8,128)(2,1)S(1)} %get-tuple-element.8.refs_0_, bf16[2048,2048]{1,0:T(8,128)(2,1)S(1)} %get-tuple-element.9.refs_1_, f32[2048]{0:T(1024)S(1)} %bitcast.3, f32[2048]{0:T(1024)S(1)} %bitcast.4), custom_call_target="tpu_custom_call" | custom-call | tf_op jit(solution)/shard_map/pallas_call | solution.py:227
